TPU v7x, 32 devices: a whole 2x2x4 slice. The times are simulated.
32 devices in a mesh: blk: 8 (over z, y), dp: 4 (over x, core).
Axes of the slice: x: 2, y: 2, z: 4, core: 2. Of those that a mesh axis runs over, the one named last changes fastest.
Arguments:
- memory: float32 [65536, 172], P(('blk', 'dp')), may hold values from -3 to 3
- src: int32 [2, 4096], P(None, ('blk', 'dp')), may hold values from 0 to 2047, as said below
- dst: int32 [2, 4096], P(None, ('blk', 'dp')), may hold values from 0 to 2047, as said below
- negative: int32 [2, 4096], P(None, ('blk', 'dp')), may hold values from 0 to 2047
- event_time: int32 [2, 4096], P(None, ('blk', 'dp')), may hold values from 0 to 1023
- neighbours: int32 [2, 10, 12288], P(None, None, ('blk', 'dp')), may hold values from 0 to 2047
- neighbour_time: int32 [2, 10, 12288], P(None, None, ('blk', 'dp')), may hold values from 0 to 1023
- time_omega: float32 [100], replicated, may hold values from 0.001 to 1
- w_input: float32 [444, 516], replicated, may hold values from -0.25 to 0.25
- w_hidden: float32 [172, 516], replicated, may hold values from -0.4375 to 0.4375
- gru_bias: float32 [2, 516], replicated, may hold values from -3 to 3
- w_query: float32 [172, 172], replicated, may hold values from -0.4807515 to 0.4807515
- w_keyval: float32 [272, 344], replicated, may hold values from -0.7508627 to 0.7508627
- w_decode: float32 [172], replicated, may hold values from -0.875 to 0.875
Outputs:
- memory_out: float32 [65536, 172], P(('blk', 'dp'))
- losses: float32 [2], replicated
- w_input_out: float32 [444, 516], replicated
- w_hidden_out: float32 [172, 516], replicated
- gru_bias_out: float32 [2, 516], replicated
- w_query_out: float32 [172, 172], replicated
- w_keyval_out: float32 [272, 344], replicated
- w_decode_out: float32 [172], replicated
Inputs may be any that keep to these rules, and one draw needn't show every extreme that they name: In each step and event block, the 128 src and 128 dst entries are 256 different rows. `dst`: different from every src entry of the same step and event block, and from each other.
All inputs are finite; a program needn't handle non-finite values.
Results may differ from a plain program's by a relative error of at most 0.00012.
Values sent between devices are 32-bit elements; how exact they have to be, the bound alone decides.
No kernel may reach another device: no remote copies, remote signals or barrier semaphores. Data moves between devices by JAX's collectives and lax.ppermute only.
A program may use at most 128 MiB of HBM per device.

v0:
```python
import jax
import jax.numpy as jnp
from jax import lax
from jax.sharding import PartitionSpec as P

HEADS = 2
STEPS = 2
rate = 0.25
exact = lax.Precision.HIGHEST


def passed_along(shard, axis, by):
    devices = lax.axis_size(axis)
    return lax.ppermute(shard, axis, [(i, (i + by) % devices) for i in range(devices)])


def step_loss(params, memory, src_ids, dst_ids, neg_ids, times, nbr_ids, nbr_times, omega, count):
    w_input, w_hidden, gru_bias, w_query, w_keyval, w_decode = params
    width = memory.shape[1]
    events = src_ids.shape[0]
    h_src = memory[src_ids]
    h_dst = memory[dst_ids]
    stamp = times.astype(jnp.float32)
    tenc = jnp.cos(stamp[:, None] * omega[None, :])
    inputs = jnp.concatenate(
        [jnp.concatenate([h_src, h_dst, tenc], 1), jnp.concatenate([h_dst, h_src, tenc], 1)], 0
    )
    hidden = jnp.concatenate([h_src, h_dst], 0)
    gate_in = (
        jnp.dot(inputs, w_input, precision=exact, preferred_element_type=jnp.float32) + gru_bias[0]
    )
    gate_hid = (
        jnp.dot(hidden, w_hidden, precision=exact, preferred_element_type=jnp.float32) + gru_bias[1]
    )
    reset = jax.nn.sigmoid(gate_in[:, :width] + gate_hid[:, :width])
    update = jax.nn.sigmoid(gate_in[:, width : 2 * width] + gate_hid[:, width : 2 * width])
    cand = jnp.tanh(gate_in[:, 2 * width :] + reset * gate_hid[:, 2 * width :])
    fresh = (1.0 - update) * cand + update * hidden
    touched = jnp.concatenate([src_ids, dst_ids], 0)
    updated = memory.at[touched].set(fresh)
    query_ids = jnp.concatenate([src_ids, dst_ids, neg_ids], 0)
    query_mem = updated[query_ids]
    rows = query_ids.shape[0]
    row_time = jnp.concatenate([stamp, stamp, stamp], 0)
    nbr_mem = updated[nbr_ids]
    delta = row_time[None, :] - nbr_times.astype(jnp.float32)
    nenc = jnp.cos(delta[:, :, None] * omega[None, None, :])
    key_in = jnp.concatenate([nbr_mem, nenc], 2)
    count_nbr = key_in.shape[0]
    keyval = jnp.dot(
        key_in.reshape(count_nbr * rows, -1),
        w_keyval,
        precision=exact,
        preferred_element_type=jnp.float32,
    )
    keyval = keyval.reshape(count_nbr, rows, 2 * width)
    query = jnp.dot(query_mem, w_query, precision=exact, preferred_element_type=jnp.float32)
    head_size = width // HEADS
    keys = keyval[:, :, :width].reshape(count_nbr, rows, HEADS, head_size)
    values = keyval[:, :, width:].reshape(count_nbr, rows, HEADS, head_size)
    query = query.reshape(rows, HEADS, head_size)
    scores = jnp.sum(keys * query[None], -1) / jnp.sqrt(jnp.float32(head_size))
    top = jnp.max(scores, 0, keepdims=True)
    probs = jnp.exp(scores - top)
    probs = probs / jnp.sum(probs, 0, keepdims=True)
    attn = jnp.sum(probs[:, :, :, None] * values, 0).reshape(rows, width)
    embed = query_mem + attn
    e_src = embed[:events]
    e_dst = embed[events : 2 * events]
    e_neg = embed[2 * events :]
    pos = jnp.sum(e_src * e_dst * w_decode[None, :], 1)
    neg = jnp.sum(e_src * e_neg * w_decode[None, :], 1)
    loss = jnp.sum(jax.nn.softplus(-pos) + jax.nn.softplus(neg)) / count
    return (loss, (updated, fresh))


def summed_terms(grads, loss):
    result = lax.psum(tuple(grads) + (loss,), ("blk", "dp"))
    return (tuple(result[:-1]), result[-1])


def on_device(
    memory,
    src,
    dst,
    negative,
    event_time,
    neighbours,
    neighbour_time,
    time_omega,
    w_input,
    w_hidden,
    gru_bias,
    w_query,
    w_keyval,
    w_decode,
):
    params = (w_input, w_hidden, gru_bias, w_query, w_keyval, w_decode)
    count = jnp.float32(src.shape[1] * lax.axis_size("blk") * lax.axis_size("dp"))
    losses = []
    for step in range(STEPS):
        current = memory
        fn = lambda p: step_loss(
            p,
            current,
            src[step],
            dst[step],
            negative[step],
            event_time[step],
            neighbours[step],
            neighbour_time[step],
            time_omega,
            count,
        )
        loss, back, extra = jax.vjp(fn, params, has_aux=True)
        updated, fresh = extra
        grads = back(jnp.float32(1.0))[0]
        sums, total = summed_terms(grads, loss)
        params = tuple((p - rate * g for p, g in zip(params, sums)))
        losses.append(total)
        memory = passed_along(updated, "blk", 1)
    return (
        memory,
        jnp.stack(losses),
        params[0],
        params[1],
        params[2],
        params[3],
        params[4],
        params[5],
    )


def solution(mesh):
    return jax.shard_map(
        on_device,
        mesh=mesh,
        in_specs=(
            P(("blk", "dp"), None),
            P(None, ("blk", "dp")),
            P(None, ("blk", "dp")),
            P(None, ("blk", "dp")),
            P(None, ("blk", "dp")),
            P(None, None, ("blk", "dp")),
            P(None, None, ("blk", "dp")),
            P(),
            P(),
            P(),
            P(),
            P(),
            P(),
            P(),
        ),
        out_specs=(P(("blk", "dp"), None), P(), P(), P(), P(), P(), P(), P()),
        check_vma=False,
    )
```

profile of v0, /device:TPU:0, one launch (start us, length us, event | category | flops | bytes accessed | tf_op | source)
XLA Modules:
  0.0 648.8 jit_solution(14372013255026179732)
XLA Ops:
  47.1 10.0 %gather_fusion.6 = f32[3840,172]{1,0:T(8,128)} fusion(f32[2048,172]{1,0:T(8,128)S(1)} %scatter_fusion, s32[4096]{0:T(1024)S(1)} %pad_clamp_fusion.1), kind=kCustom, calls=%fused_computation.6 | custom fusion | bytes 5299200 | tf_op jit(solution)/shard_map/jvp()/gather | solution.py:45
  60.7 12.4 %multiply_cosine_fusion = (f32[10,384,100]{1,2,0:T(8,128)}, f32[10,384,100]{1,2,0:T(8,128)S(1)}) fusion(f32[10,384]{1,0:T(8,128)S(1)} %fusion.64, f32[100]{0:T(128)} %param.22, f32[10,384]{1,0:T(8,128)S(1)} %fusion.66), kind=kLoop, calls=%fused_computation.40 | loop fusion | flops 768000 | bytes 3103120 | tf_op jit(solution)/shard_map/jvp()/cos | solution.py:47
  73.1 9.6 %fusion.5 = f32[10,384,344]{1,2,0:T(8,128)S(1)} fusion(f32[10,384,100]{1,2,0:T(8,128)S(1)} %get-tuple-element.135, f32[10,384,172]{1,2,0:T(8,128)S(1)} %copy.82, f32[272,344]{1,0:T(8,128)S(1)} %copy-done.18), kind=kOutput, calls=%fused_computation.29 | convolution fusion | flops 4312657920 | bytes 9836032 | tf_op jit(solution)/shard_map/jvp()/dot_general | solution.py:50
  95.7 3.8 multiply_reduce_fusion.6
  112.4 4.6 multiply_reduce_fusion.4
  119.9 10.7 %fusion.7 = f32[272,344]{1,0:T(8,128)} fusion(f32[10,384,172]{1,2,0:T(8,128)} %get-tuple-element.101, f32[10,384,172]{1,2,0:T(8,128)} %broadcast_multiply_fusion.3, f32[10,384,100]{1,2,0:T(8,128)} %copy-done.14, f32[10,384,172]{1,2,0:T(8,128)S(1)} %copy-done.6), kind=kOutput, calls=%fused_computation.51 | convolution fusion | flops 4313978880 | bytes 9836032 | tf_op jit(solution)/shard_map/transpose(jvp())/dot_general | solution.py:50
  130.6 11.5 %fusion.1 = f32[10,384,172]{2,1,0:T(8,128)} fusion(f32[10,384,172]{1,2,0:T(8,128)S(1)} %copy-done.10, f32[10,384,172]{1,2,0:T(8,128)S(1)} %copy-done.8, f32[272,344,1]{1,0,2:T(8,128)S(1)} %bitcast.110), kind=kOutput, calls=%fused_computation.23 | convolution fusion | flops 2727782400 | bytes 8318976 | tf_op jit(solution)/shard_map/transpose(jvp())/split | solution.py:48
  142.2 21.5 %scatter_custom_fusion.3 = f32[2048,172]{1,0:T(8,128)S(1)} fusion(s32[3840]{0:T(1024)} %copy-done.82, f32[3840,172]{1,0:T(8,128)} %bitcast.112, f32[]{:T(128)} %constant.19.clone.1), kind=kCustom, calls=%fused_computation.62 | custom fusion | flops 660480 | bytes 1409536 | tf_op jit(solution)/shard_map/transpose(jvp())/scatter-add | solution.py:45
  163.7 4.5 scatter_custom_fusion.4
  183.0 41.2 %all-reduce.23 = (f32[2,516]{1,0:T(2,128)S(1)}, f32[172]{0:T(256)S(1)}) all-reduce(f32[2,516]{1,0:T(2,128)S(1)} %pad_add_fusion.25, f32[172]{0:T(256)S(1)} %add_any.104), channel_id=1, replica_groups=mesh['blk'=8,'dp'=4] {'blk','dp'}, use_global_device_ids=true, to_apply=%region_19.21 | all-reduce | flops 1204 | bytes 9632 | tf_op jit(solution)/shard_map/psum | solution.py:78
  227.8 87.3 %all-reduce.31.cloned.1.call-done = (f32[444,516]{0,1:T(8,128)}, f32[172,516]{1,0:T(8,128)}, f32[272,344]{1,0:T(8,128)}, f32[172,172]{1,0:T(8,128)}) async-done(((f32[444,516]{0,1:T(8,128)}, f32[172,516]{1,0:T(8,128)}, f32[272,344]{1,0:T(8,128)}, f32[172,172]{1,0:T(8,128)}), (f32[444,516]{0,1:T(8,128)}, f32[172,516]{1,0:T(8,128)}, f32[272,344]{1,0:T(8,128)}, ...) | async-done | bytes 1764048 | tf_op jit(solution)/shard_map/psum | solution.py:78
  345.5 10.5 %gather_fusion.10 = f32[3840,172]{1,0:T(8,128)} fusion(f32[2048,172]{1,0:T(8,128)S(1)} %scatter_fusion.1, s32[4096]{0:T(1024)} %pad_clamp_fusion), kind=kCustom, calls=%fused_computation.10 | custom fusion | bytes 5299200 | tf_op jit(solution)/shard_map/jvp()/gather | solution.py:45
  356.1 5.1 copy.94
  361.2 10.7 %fusion.4 = f32[10,384,344]{1,2,0:T(8,128)S(1)} fusion(f32[272,344,1]{1,0,2:T(8,128)} %fusion.58, f32[10,384,100]{1,2,0:T(8,128)} %get-tuple-element.134, f32[10,384,172]{1,2,0:T(8,128)} %copy.94), kind=kOutput, calls=%fused_computation.28 | convolution fusion | flops 4312657920 | bytes 9836032 | tf_op jit(solution)/shard_map/jvp()/dot_general | solution.py:50
  384.3 3.7 mul.489
  388.0 4.7 fusion.115
  406.9 3.9 broadcast_in_dim.101
  416.0 7.8 %fusion.6 = f32[272,344]{1,0:T(8,128)} fusion(f32[10,384,172]{1,2,0:T(8,128)S(1)} %get-tuple-element.99, f32[10,384,172]{1,2,0:T(8,128)S(1)} %copy-done.9, f32[10,384,100]{1,2,0:T(8,128)S(1)} %copy-done.13, f32[10,384,172]{1,2,0:T(8,128)S(1)} %copy-done.7), kind=kOutput, calls=%fused_computation.50 | convolution fusion | flops 4313978880 | bytes 9836032 | tf_op jit(solution)/shard_map/transpose(jvp())/dot_general | solution.py:50
  423.8 11.8 %fusion.3 = f32[10,384,172]{2,1,0:T(8,128)} fusion(f32[10,384,172]{1,2,0:T(8,128)S(1)} %get-tuple-element.99, f32[10,384,172]{1,2,0:T(8,128)S(1)} %copy-done.9, f32[272,344,1]{1,0,2:T(8,128)S(1)} %copy-done.29), kind=kOutput, calls=%fused_computation.25 | convolution fusion | flops 2727782400 | bytes 8318976 | tf_op jit(solution)/shard_map/transpose(jvp())/split | solution.py:48
  436.5 22.2 %scatter_custom_fusion.6 = f32[2048,172]{1,0:T(8,128)} fusion(s32[3840]{0:T(1024)} %copy-done.81, f32[3840,172]{1,0:T(8,128)} %bitcast.111, f32[]{:T(128)} %constant.19.clone.1), kind=kCustom, calls=%fused_computation.58 | custom fusion | flops 660480 | bytes 1409536 | tf_op jit(solution)/shard_map/transpose(jvp())/scatter-add | solution.py:45
  458.8 4.7 scatter_custom_fusion.7
  463.5 3.8 add_any.112
  486.0 67.1 %all-reduce.22 = (f32[1]{0:T(128)}, f32[1]{0:T(128)}, f32[2,516]{1,0:T(2,128)S(1)}, f32[172]{0:T(256)S(1)}) all-reduce(f32[1]{0:T(128)} %bitcast.27, f32[1]{0:T(128)} %bitcast.20, f32[2,516]{1,0:T(2,128)S(1)} %pad_add_fusion.24, f32[172]{0:T(256)S(1)} %add_any.119), channel_id=1, replica_groups=mesh['blk'=8,'dp'=4] {'blk','dp'}, use_global_device_ids=true, to_apply=%region_36.38 | all-reduce | flops 1206 | bytes 9648 | tf_op jit(solution)/shard_map/psum | solution.py:78
  556.1 75.7 %all-reduce.29.cloned.1.call-done = (f32[444,516]{0,1:T(8,128)}, f32[172,516]{1,0:T(8,128)}, f32[172,172]{1,0:T(8,128)}, f32[272,344]{1,0:T(8,128)}) async-done(((f32[444,516]{0,1:T(8,128)}, f32[172,516]{1,0:T(8,128)}, f32[172,172]{1,0:T(8,128)}, f32[272,344]{1,0:T(8,128)}), (f32[444,516]{0,1:T(8,128)}, f32[172,516]{1,0:T(8,128)}, f32[172,172]{1,0:T(8,128)}, ...) | async-done | bytes 1764048 | tf_op jit(solution)/shard_map/psum | solution.py:78
  (406 shorter events, 182.3 us)
Async XLA Ops:
  7.2 308.0 %all-reduce.31.cloned.1.call-start = ((), (), s32[]{:S(2)}) async-start(), calls=%async_computation.1 | async-start | bytes 4227072 | tf_op jit(solution)/shard_map/psum | solution.py:78
  7.2 25.1 %copy-start.90 = (u32[256]{0:T(256)}, u32[256]{0:T(256)S(1)}, u32[]{:S(2)}) copy-start(u32[256]{0:T(256)S(1)} %iota_add_fusion) | copy-start | bytes 3076
  15.5 16.8 %copy-start.33 = (f32[128,172]{0,1:T(8,128)}, f32[128,172]{0,1:T(8,128)S(1)}, u32[]{:S(2)}) copy-start(f32[128,172]{0,1:T(8,128)S(1)} %copy.73) | copy-start | bytes 264196
  38.6 278.4 %collective-permute-start = (f32[2048,172]{0,1:T(8,128)}, f32[2048,172]{0,1:T(8,128)}, u32[]{:S(2)}, u32[]{:S(2)}) collective-permute-start(f32[2048,172]{0,1:T(8,128)} %copy.75), channel_id=1, source_target_pairs={{0,4},{4,8},{8,12},{12,16},{16,20},{20,24},{24,28},{28,0},{1,5},{5... | collective-permute-start | bytes 4227080 | tf_op jit(solution)/shard_map/ppermute | solution.py:14
  60.6 22.1 %copy-start.5 = (f32[10,384,172]{1,2,0:T(8,128)}, f32[10,384,172]{1,2,0:T(8,128)S(1)}, u32[]{:S(2)}) copy-start(f32[10,384,172]{1,2,0:T(8,128)S(1)} %copy.82) | copy-start | bytes 7925764
  178.6 45.5 %copy-start.109 = (s32[128]{0:T(128)S(1)}, s32[128]{0:T(128)}, u32[]{:S(2)}) copy-start(s32[128]{0:T(128)} %get-tuple-element.130) | copy-start | bytes 1540
  178.7 46.1 %copy-start.108 = (s32[128]{0:T(128)S(1)}, s32[128]{0:T(128)}, u32[]{:S(2)}) copy-start(s32[128]{0:T(128)} %get-tuple-element.128) | copy-start | bytes 1540
  178.7 46.7 %copy-start.113 = (s32[128]{0:T(128)S(1)}, s32[128]{0:T(128)}, u32[]{:S(2)}) copy-start(s32[128]{0:T(128)} %get-tuple-element.120) | copy-start | bytes 1540
  178.7 46.7 %copy-start.114 = (s32[128]{0:T(128)S(1)}, s32[128]{0:T(128)}, u32[]{:S(2)}) copy-start(s32[128]{0:T(128)} %get-tuple-element.142) | copy-start | bytes 1540
  178.7 453.1 %all-reduce.29.cloned.1.call-start = ((), (), s32[]{:S(2)}) async-start(), calls=%async_computation | async-start | bytes 4227072 | tf_op jit(solution)/shard_map/psum | solution.py:78
  179.0 48.2 %copy-start.89 = (f32[2,516]{1,0:T(2,128)S(1)}, f32[2,516]{1,0:T(2,128)}, u32[]{:S(2)}) copy-start(f32[2,516]{1,0:T(2,128)} %param.25) | copy-start | bytes 12388
  179.0 48.2 %copy-start.97 = (f32[172]{0:T(256)S(1)}, f32[172]{0:T(256)}, u32[]{:S(2)}) copy-start(f32[172]{0:T(256)} %param.28) | copy-start | bytes 2068
  179.1 137.8 %copy-start.98 = (s32[1024]{0:T(1024)}, s32[1024]{0:T(1024)S(1)}, u32[]{:S(2)}) copy-start(s32[1024]{0:T(1024)S(1)} %pad_clamp_fusion.6) | copy-start | bytes 12292
  181.2 135.8 %copy-start.3 = (u32[2048,172]{1,0:T(8,128)}, u32[2048,172]{1,0:T(8,128)S(1)}, u32[]{:S(2)}) copy-start(u32[2048,172]{1,0:T(8,128)S(1)} %scatter_custom_fusion) | copy-start | bytes 4227076
  181.2 138.6 %copy-start.81 = (s32[3840]{0:T(1024)}, s32[3840]{0:T(1024)S(1)}, u32[]{:S(2)}) copy-start(s32[3840]{0:T(1024)S(1)} %reshape.961) | copy-start | bytes 46084
  183.0 136.8 %copy-start.100 = (s32[384]{0:T(512)}, s32[384]{0:T(512)S(1)}, u32[]{:S(2)}) copy-start(s32[384]{0:T(512)S(1)} %fusion.70) | copy-start | bytes 4612
  227.2 92.6 %copy-start.85 = (f32[2,516]{1,0:T(2,128)}, f32[2,516]{1,0:T(2,128)S(1)}, u32[]{:S(2)}) copy-start(f32[2,516]{1,0:T(2,128)S(1)} %multiply_subtract_fusion.11) | copy-start | bytes 12388
  480.2 72.9 %copy-start.93 = (f32[172]{0:T(256)S(1)}, f32[172]{0:T(256)}, u32[]{:S(2)}) copy-start(f32[172]{0:T(256)} %multiply_subtract_fusion.13) | copy-start | bytes 2068
  480.2 75.3 %copy-start.86 = (f32[2,516]{1,0:T(2,128)S(1)}, f32[2,516]{1,0:T(2,128)}, u32[]{:S(2)}) copy-start(f32[2,516]{1,0:T(2,128)} %copy-done.85) | copy-start | bytes 12388
  480.3 151.6 %copy-start.25 = (f32[172,172]{1,0:T(8,128)S(1)}, f32[172,172]{1,0:T(8,128)}, u32[]{:S(2)}) copy-start(f32[172,172]{1,0:T(8,128)} %param.26) | copy-start | bytes 355012
  482.5 153.2 %copy-start.28 = (f32[172,516]{1,0:T(8,128)S(1)}, f32[172,516]{1,0:T(8,128)}, u32[]{:S(2)}) copy-start(f32[172,516]{1,0:T(8,128)} %param.24) | copy-start | bytes 1065028
  482.5 153.2 %copy-start.42 = (f32[172,516]{1,0:T(8,128)S(1)}, f32[172,516]{1,0:T(8,128)}, u32[]{:S(2)}) copy-start(f32[172,516]{1,0:T(8,128)} %get-tuple-element.73) | copy-start | bytes 1065028
  482.5 155.0 %copy-start.26 = (f32[444,516]{0,1:T(8,128)S(1)}, f32[444,516]{0,1:T(8,128)}, u32[]{:S(2)}) copy-start(f32[444,516]{0,1:T(8,128)} %get-tuple-element.72) | copy-start | bytes 2749252
  482.5 156.4 %collective-permute-start.1 = (f32[2048,172]{0,1:T(8,128)}, f32[2048,172]{0,1:T(8,128)}, u32[]{:S(2)}, u32[]{:S(2)}) collective-permute-start(f32[2048,172]{0,1:T(8,128)} %copy.91), channel_id=1, source_target_pairs={{0,4},{4,8},{8,12},{12,16},{16,20},{20,24},{24,28},{28,0},{1,5},{5... | collective-permute-start | bytes 4227080 | tf_op jit(solution)/shard_map/ppermute | solution.py:14
  (98 other events, 438.4 us)
Sparse Core Ops, SparseCore 0:
  178.7 136.3 all-reduce.30
  480.4 151.4 all-reduce.28
where the time goes:
time: 657 us; the launch traced here: 649 us
  waiting for transfers between devices  163 us (25%)
  other arithmetic  141 us (21%)
  local copies, waits for them, and re-layouts  129 us (20%)
  blocking collectives  108 us (16%)
  matrix products  85.7 us (13%)
  between operations  17.4 us (3%)
    psum x2, waiting for transfers between devices, summed_terms(): result = lax.psum(tuple(grads) + (loss,), ('blk', 'dp'))  163 us
    psum x2, blocking collectives, summed_terms(): result = lax.psum(tuple(grads) + (loss,), ('blk', 'dp'))  108 us
    scatter-add x2, other arithmetic, step_loss(): nbr_mem = updated[nbr_ids]  43.8 us
    dot_general x4, matrix products, step_loss(): jnp.dot(key_in.reshape(count_nbr * rows, -1), w_keyval, precision=exact,...  38.8 us
    gather x4, local copies, waits for them, and re-layouts, step_loss(): nbr_mem = updated[nbr_ids]  29.1 us
    split x2, matrix products, step_loss(): key_in = jnp.concatenate([nbr_mem, nenc], 2)  23.3 us
    gather x8, local copies, waits for them, and re-layouts, step_loss(): updated = memory.at[touched].set(fresh)  14.9 us
    unnamed x238, local copies, waits for them, and re-layouts  13.9 us
  transfers between devices with their start and end apart: 4, of which 2 were waited for; matrix products, arithmetic and copies ran while one was open for 24% of the time, Pallas kernels for 0%

commit v1 on v0

--- a/solution.py
+++ b/solution.py
@@ -7,6 +7,9 @@
 STEPS = 2
 rate = 0.25
 exact = lax.Precision.HIGHEST
+meet_figure = lambda x_part, row_axis, axis_tag: jax.lax.psum(
+    jax.lax.psum(x_part, axis_name=row_axis), axis_tag
+)
 
 
 def passed_along(shard, axis, by):
@@ -75,7 +78,7 @@
 
 
 def summed_terms(grads, loss):
-    result = lax.psum(tuple(grads) + (loss,), ("blk", "dp"))
+    result = meet_figure(tuple(grads) + (loss,), "dp", "blk")
     return (tuple(result[:-1]), result[-1])
 
 

time: 657 us -> 724 us (1.10)
  waiting for transfers between devices: 163 us -> 215 us
  local copies, waits for them, and re-layouts: 129 us -> 144 us
  blocking collectives: 108 us -> 94.1 us
  other arithmetic: 141 us -> 152 us
    psum x2 -> x4, waiting for transfers between devices: 163 us -> 215 us  [the longest x2 115 us: jax.lax.psum(jax.lax.psum(x_part, axis_name=row_axis), axis_tag)]
    psum x2 -> x4, blocking collectives: 108 us -> 94.1 us  [the longest x2 81.5 us: jax.lax.psum(jax.lax.psum(x_part, axis_name=row_axis), axis_tag)]
    unnamed x238 -> x244, local copies, waits for them, and re-layouts: 13.9 us -> 15 us
  transfers between devices with their start and end apart: 4 -> 6, of which waited for: 2 -> 4; matrix products, arithmetic and copies ran while one was open for 24% -> 4% of each run, Pallas kernels for 0% -> 0%
where the time goes in v1:
time: 724 us; the launch traced here: 715 us
  waiting for transfers between devices  215 us (30%)
  other arithmetic  152 us (21%)
  local copies, waits for them, and re-layouts  144 us (20%)
  blocking collectives  94.1 us (13%)
  matrix products  88.7 us (12%)
  between operations  17 us (2%)
    psum x2, waiting for transfers between devices, jax.lax.psum(jax.lax.psum(x_part, axis_name=row_axis), axis_tag)  115 us
    psum x2, waiting for transfers between devices, jax.lax.psum(x_part, axis_name=row_axis)  99.2 us
    psum x2, blocking collectives, jax.lax.psum(jax.lax.psum(x_part, axis_name=row_axis), axis_tag)  81.5 us
    scatter-add x2, other arithmetic, step_loss(): nbr_mem = updated[nbr_ids]  44.7 us
    dot_general x4, matrix products, step_loss(): jnp.dot(key_in.reshape(count_nbr * rows, -1), w_keyval, precision=exact,...  39.2 us
    gather x4, local copies, waits for them, and re-layouts, step_loss(): nbr_mem = updated[nbr_ids]  31.4 us
    split x2, matrix products, step_loss(): key_in = jnp.concatenate([nbr_mem, nenc], 2)  23.3 us
    gather x8, local copies, waits for them, and re-layouts, step_loss(): updated = memory.at[touched].set(fresh)  17.2 us
  transfers between devices with their start and end apart: 6, of which 4 were waited for; matrix products, arithmetic and copies ran while one was open for 4% of the time, Pallas kernels for 0%

profile of v1, /device:TPU:0, one launch (start us, length us, event | category | flops | bytes accessed | tf_op | source)
XLA Modules:
  0.0 715.0 jit_solution(16985010035170524822)
XLA Ops:
  52.1 10.6 %gather_fusion.6 = f32[3840,172]{1,0:T(8,128)} fusion(f32[2048,172]{1,0:T(8,128)S(1)} %scatter_fusion, s32[4096]{0:T(1024)} %pad_clamp_fusion.1), kind=kCustom, calls=%fused_computation.6 | custom fusion | bytes 5299200 | tf_op jit(solution)/shard_map/jvp()/gather | solution.py:48
  62.6 5.1 copy.82
  69.4 12.1 %multiply_cosine_fusion = (f32[10,384,100]{1,2,0:T(8,128)}, f32[10,384,100]{1,2,0:T(8,128)S(1)}) fusion(f32[10,384]{1,0:T(8,128)S(1)} %fusion.64, f32[100]{0:T(128)} %param.22, f32[10,384]{1,0:T(8,128)S(1)} %fusion.66), kind=kLoop, calls=%fused_computation.40 | loop fusion | flops 768000 | bytes 3103120 | tf_op jit(solution)/shard_map/jvp()/cos | solution.py:50
  81.6 9.6 %fusion.5 = f32[10,384,344]{1,2,0:T(8,128)S(1)} fusion(f32[10,384,100]{1,2,0:T(8,128)S(1)} %get-tuple-element.149, f32[10,384,172]{1,2,0:T(8,128)S(1)} %copy-done.6, f32[272,344]{1,0:T(8,128)S(1)} %copy-done.16), kind=kOutput, calls=%fused_computation.29 | convolution fusion | flops 4312657920 | bytes 9836032 | tf_op jit(solution)/shard_map/jvp()/dot_general | solution.py:53
  107.4 4.7 multiply_reduce_fusion.6
  137.9 11.1 %fusion.7 = f32[272,344]{1,0:T(8,128)} fusion(f32[10,384,172]{1,2,0:T(8,128)} %get-tuple-element.115, f32[10,384,172]{1,2,0:T(8,128)} %broadcast_multiply_fusion.3, f32[10,384,100]{1,2,0:T(8,128)} %copy-done.13, f32[10,384,172]{1,2,0:T(8,128)} %copy.82), kind=kOutput, calls=%fused_computation.51 | convolution fusion | flops 4313978880 | bytes 9836032 | tf_op jit(solution)/shard_map/transpose(jvp())/dot_general | solution.py:53
  149.1 11.5 %fusion.1 = f32[10,384,172]{2,1,0:T(8,128)} fusion(f32[10,384,172]{1,2,0:T(8,128)S(1)} %copy-done.10, f32[10,384,172]{1,2,0:T(8,128)S(1)} %copy-done.8, f32[272,344,1]{1,0,2:T(8,128)S(1)} %bitcast.110), kind=kOutput, calls=%fused_computation.23 | convolution fusion | flops 2727782400 | bytes 8318976 | tf_op jit(solution)/shard_map/transpose(jvp())/split | solution.py:51
  160.6 22.4 %scatter_custom_fusion.3 = f32[2048,172]{1,0:T(8,128)} fusion(s32[3840]{0:T(1024)} %copy-done.85, f32[3840,172]{1,0:T(8,128)} %bitcast.112, f32[]{:T(128)} %constant.19.clone.1), kind=kCustom, calls=%fused_computation.62 | custom fusion | flops 660480 | bytes 1409536 | tf_op jit(solution)/shard_map/transpose(jvp())/scatter-add | solution.py:48
  211.0 48.0 %all-reduce.41.cloned.1.call-done = (f32[444,516]{0,1:T(8,128)}, f32[172,516]{1,0:T(8,128)}, f32[272,344]{1,0:T(8,128)}, f32[172,172]{1,0:T(8,128)}) async-done(((f32[444,516]{0,1:T(8,128)}, f32[172,516]{1,0:T(8,128)}, f32[272,344]{1,0:T(8,128)}, f32[172,172]{1,0:T(8,128)}), (f32[444,516]{0,1:T(8,128)}, f32[172,516]{1,0:T(8,128)}, f32[272,344]{1,0:T(8,128)}, ...) | async-done | bytes 1764048 | tf_op jit(solution)/shard_map/psum | solution.py:11
  263.2 5.9 all-reduce.27
  269.1 23.3 %all-reduce.23 = (f32[2,516]{1,0:T(2,128)S(1)}, f32[172]{0:T(256)S(1)}) all-reduce(f32[2,516]{1,0:T(2,128)S(1)} %get-tuple-element.80, f32[172]{0:T(256)S(1)} %get-tuple-element.81), channel_id=1, replica_groups=mesh['blk'=8,'dp'=4] {'blk'}, use_global_device_ids=true, to_apply=%region_21.23 | all-reduce | flops 1204 | bytes 9632 | tf_op jit(solution)/shard_map/psum | solution.py:10
  306.2 60.2 %all-reduce.37.cloned.1.call-done = (f32[444,516]{0,1:T(8,128)}, f32[172,516]{1,0:T(8,128)}, f32[272,344]{1,0:T(8,128)}, f32[172,172]{1,0:T(8,128)}) async-done(((f32[444,516]{0,1:T(8,128)}, f32[172,516]{1,0:T(8,128)}, f32[272,344]{1,0:T(8,128)}, f32[172,172]{1,0:T(8,128)}), (f32[444,516]{0,1:T(8,128)}, f32[172,516]{1,0:T(8,128)}, f32[272,344]{1,0:T(8,128)}, ...) | async-done | bytes 1764048 | tf_op jit(solution)/shard_map/psum | solution.py:10
  384.3 10.6 %gather_fusion.10 = f32[3840,172]{1,0:T(8,128)} fusion(f32[2048,172]{1,0:T(8,128)S(1)} %scatter_fusion.1, s32[4096]{0:T(1024)} %pad_clamp_fusion), kind=kCustom, calls=%fused_computation.10 | custom fusion | bytes 5299200 | tf_op jit(solution)/shard_map/jvp()/gather | solution.py:48
  394.9 5.1 copy.94
  400.0 10.7 %fusion.4 = f32[10,384,344]{1,2,0:T(8,128)S(1)} fusion(f32[272,344,1]{1,0,2:T(8,128)} %fusion.58, f32[10,384,100]{1,2,0:T(8,128)} %get-tuple-element.148, f32[10,384,172]{1,2,0:T(8,128)} %copy.94), kind=kOutput, calls=%fused_computation.28 | convolution fusion | flops 4312657920 | bytes 9836032 | tf_op jit(solution)/shard_map/jvp()/dot_general | solution.py:53
  426.8 4.7 fusion.115
  454.8 7.8 %fusion.6 = f32[272,344]{1,0:T(8,128)} fusion(f32[10,384,172]{1,2,0:T(8,128)S(1)} %get-tuple-element.113, f32[10,384,172]{1,2,0:T(8,128)S(1)} %copy-done.9, f32[10,384,100]{1,2,0:T(8,128)S(1)} %copy-done.12, f32[10,384,172]{1,2,0:T(8,128)S(1)} %copy-done.7), kind=kOutput, calls=%fused_computation.50 | convolution fusion | flops 4313978880 | bytes 9836032 | tf_op jit(solution)/shard_map/transpose(jvp())/dot_general | solution.py:53
  462.6 11.7 %fusion.3 = f32[10,384,172]{2,1,0:T(8,128)} fusion(f32[10,384,172]{1,2,0:T(8,128)S(1)} %get-tuple-element.113, f32[10,384,172]{1,2,0:T(8,128)S(1)} %copy-done.9, f32[272,344,1]{1,0,2:T(8,128)S(1)} %copy-done.26), kind=kOutput, calls=%fused_computation.25 | convolution fusion | flops 2727782400 | bytes 8318976 | tf_op jit(solution)/shard_map/transpose(jvp())/split | solution.py:51
  475.3 22.2 %scatter_custom_fusion.6 = f32[2048,172]{1,0:T(8,128)} fusion(s32[3840]{0:T(1024)} %copy-done.84, f32[3840,172]{1,0:T(8,128)} %bitcast.111, f32[]{:T(128)} %constant.19.clone.1), kind=kCustom, calls=%fused_computation.58 | custom fusion | flops 660480 | bytes 1409536 | tf_op jit(solution)/shard_map/transpose(jvp())/scatter-add | solution.py:48
  497.5 4.7 scatter_custom_fusion.7
  519.0 51.2 %all-reduce.39.cloned.1.call-done = (f32[444,516]{0,1:T(8,128)}, f32[172,516]{1,0:T(8,128)}, f32[172,172]{1,0:T(8,128)}, f32[272,344]{1,0:T(8,128)}) async-done(((f32[444,516]{0,1:T(8,128)}, f32[172,516]{1,0:T(8,128)}, f32[172,172]{1,0:T(8,128)}, f32[272,344]{1,0:T(8,128)}), (f32[444,516]{0,1:T(8,128)}, f32[172,516]{1,0:T(8,128)}, f32[172,172]{1,0:T(8,128)}, ...) | async-done | bytes 1764048 | tf_op jit(solution)/shard_map/psum | solution.py:11
  576.1 6.8 all-reduce.26
  582.8 58.2 %all-reduce.22 = (f32[1]{0:T(128)}, f32[1]{0:T(128)}, f32[2,516]{1,0:T(2,128)S(1)}, f32[172]{0:T(256)S(1)}) all-reduce(f32[1]{0:T(128)} %bitcast.27, f32[1]{0:T(128)} %bitcast.20, f32[2,516]{1,0:T(2,128)S(1)} %get-tuple-element.78, f32[172]{0:T(256)S(1)} %get-tuple-element.79), channel_id=1, replica_groups=mesh['blk'=8,'dp'=4] {'blk'}, use_global_device_ids=true, to_apply=%region_44.46 | all-reduce | flops 1206 | bytes 9648 | tf_op jit(solution)/shard_map/psum | solution.py:10
  644.1 55.1 %all-reduce.35.cloned.1.call-done = (f32[444,516]{0,1:T(8,128)}, f32[172,516]{1,0:T(8,128)}, f32[172,172]{1,0:T(8,128)}, f32[272,344]{1,0:T(8,128)}) async-done(((f32[444,516]{0,1:T(8,128)}, f32[172,516]{1,0:T(8,128)}, f32[172,172]{1,0:T(8,128)}, f32[272,344]{1,0:T(8,128)}), (f32[444,516]{0,1:T(8,128)}, f32[172,516]{1,0:T(8,128)}, f32[172,172]{1,0:T(8,128)}, ...) | async-done | bytes 1764048 | tf_op jit(solution)/shard_map/psum | solution.py:10
  (420 shorter events, 224.5 us)
Async XLA Ops:
  7.2 251.9 %all-reduce.41.cloned.1.call-start = ((), (), s32[]{:S(2)}) async-start(), calls=%async_computation.3 | async-start | bytes 4227072 | tf_op jit(solution)/shard_map/psum | solution.py:11
  204.3 55.0 %copy-start.94 = (u32[256]{0:T(256)S(1)}, u32[256]{0:T(256)}, u32[]{:S(2)}) copy-start(u32[256]{0:T(256)} %copy-done.93) | copy-start | bytes 3076
  204.3 162.1 %all-reduce.37.cloned.1.call-start = ((), (), s32[]{:S(2)}) async-start(), calls=%async_computation.1 | async-start | bytes 4227072 | tf_op jit(solution)/shard_map/psum | solution.py:10
  206.0 55.3 %copy-start.83 = (s32[10,384]{1,0:T(8,128)S(1)}, s32[10,384]{1,0:T(8,128)}, u32[]{:S(2)}) copy-start(s32[10,384]{1,0:T(8,128)} %get-tuple-element.56) | copy-start | bytes 46084
  206.0 88.7 %collective-permute-start = (f32[2048,172]{0,1:T(8,128)}, f32[2048,172]{0,1:T(8,128)}, u32[]{:S(2)}, u32[]{:S(2)}) collective-permute-start(f32[2048,172]{0,1:T(8,128)} %copy.75), channel_id=1, source_target_pairs={{0,4},{4,8},{8,12},{12,16},{16,20},{20,24},{24,28},{28,0},{1,5},{5... | collective-permute-start | bytes 4227080 | tf_op jit(solution)/shard_map/ppermute | solution.py:17
  259.1 33.2 %copy-start.116 = (s32[128]{0:T(128)S(1)}, s32[128]{0:T(128)}, u32[]{:S(2)}) copy-start(s32[128]{0:T(128)} %get-tuple-element.134) | copy-start | bytes 1540
  259.2 33.7 %copy-start.114 = (s32[128]{0:T(128)S(1)}, s32[128]{0:T(128)}, u32[]{:S(2)}) copy-start(s32[128]{0:T(128)} %get-tuple-element.144) | copy-start | bytes 1540
  259.2 33.7 %copy-start.113 = (s32[128]{0:T(128)S(1)}, s32[128]{0:T(128)}, u32[]{:S(2)}) copy-start(s32[128]{0:T(128)} %get-tuple-element.142) | copy-start | bytes 1540
  259.2 34.9 %copy-start.92 = (f32[2,516]{1,0:T(2,128)S(1)}, f32[2,516]{1,0:T(2,128)}, u32[]{:S(2)}) copy-start(f32[2,516]{1,0:T(2,128)} %param.25) | copy-start | bytes 12388
  259.2 35.0 %copy-start.100 = (f32[172]{0:T(256)S(1)}, f32[172]{0:T(256)}, u32[]{:S(2)}) copy-start(f32[172]{0:T(256)} %param.28) | copy-start | bytes 2068
  259.2 311.0 %all-reduce.39.cloned.1.call-start = ((), (), s32[]{:S(2)}) async-start(), calls=%async_computation.2 | async-start | bytes 4227072 | tf_op jit(solution)/shard_map/psum | solution.py:11
  259.3 35.5 %copy-start.101 = (s32[1024]{0:T(1024)}, s32[1024]{0:T(1024)S(1)}, u32[]{:S(2)}) copy-start(s32[1024]{0:T(1024)S(1)} %pad_clamp_fusion.6) | copy-start | bytes 12292
  261.3 36.7 %copy-start.4 = (u32[2048,172]{1,0:T(8,128)}, u32[2048,172]{1,0:T(8,128)S(1)}, u32[]{:S(2)}) copy-start(u32[2048,172]{1,0:T(8,128)S(1)} %scatter_custom_fusion) | copy-start | bytes 4227076
  261.4 33.4 %copy-start.84 = (s32[3840]{0:T(1024)}, s32[3840]{0:T(1024)S(1)}, u32[]{:S(2)}) copy-start(s32[3840]{0:T(1024)S(1)} %reshape.961) | copy-start | bytes 46084
  300.4 68.0 %copy-start.51 = (f32[128,172]{1,0:T(8,128)}, f32[128,172]{1,0:T(8,128)S(1)}, u32[]{:S(2)}) copy-start(f32[128,172]{1,0:T(8,128)S(1)} %gather_fusion.5) | copy-start | bytes 264196
  303.5 68.6 %copy-start.33 = (f32[128,172]{0,1:T(8,128)}, f32[128,172]{0,1:T(8,128)S(1)}, u32[]{:S(2)}) copy-start(f32[128,172]{0,1:T(8,128)S(1)} %copy.88) | copy-start | bytes 264196
  303.6 68.5 %copy-start.35 = (f32[128,172]{0,1:T(8,128)}, f32[128,172]{0,1:T(8,128)S(1)}, u32[]{:S(2)}) copy-start(f32[128,172]{0,1:T(8,128)S(1)} %copy.89) | copy-start | bytes 264196
  303.6 64.8 %copy-start.75 = (f32[128,100]{1,0:T(8,128)S(1)}, f32[128,100]{1,0:T(8,128)}, u32[]{:S(2)}) copy-start(f32[128,100]{1,0:T(8,128)} %get-tuple-element.150) | copy-start | bytes 153604
  519.0 180.2 %all-reduce.35.cloned.1.call-start = ((), (), s32[]{:S(2)}) async-start(), calls=%async_computation | async-start | bytes 4227072 | tf_op jit(solution)/shard_map/psum | solution.py:10
  570.2 72.7 %copy-start.96 = (f32[172]{0:T(256)S(1)}, f32[172]{0:T(256)}, u32[]{:S(2)}) copy-start(f32[172]{0:T(256)} %multiply_subtract_fusion.13) | copy-start | bytes 2068
  570.2 73.3 %copy-start.91 = (f32[2,516]{1,0:T(2,128)S(1)}, f32[2,516]{1,0:T(2,128)}, u32[]{:S(2)}) copy-start(f32[2,516]{1,0:T(2,128)} %copy-done.90) | copy-start | bytes 12388
  570.2 131.1 %copy-start.22 = (f32[172,172]{1,0:T(8,128)S(1)}, f32[172,172]{1,0:T(8,128)}, u32[]{:S(2)}) copy-start(f32[172,172]{1,0:T(8,128)} %param.26) | copy-start | bytes 355012
  571.9 131.3 %copy-start.23 = (f32[444,516]{0,1:T(8,128)S(1)}, f32[444,516]{0,1:T(8,128)}, u32[]{:S(2)}) copy-start(f32[444,516]{0,1:T(8,128)} %get-tuple-element.72) | copy-start | bytes 2749252
  571.9 72.2 %collective-permute-start.1 = (f32[2048,172]{0,1:T(8,128)}, f32[2048,172]{0,1:T(8,128)}, u32[]{:S(2)}, u32[]{:S(2)}) collective-permute-start(f32[2048,172]{0,1:T(8,128)} %copy.91), channel_id=1, source_target_pairs={{0,4},{4,8},{8,12},{12,16},{16,20},{20,24},{24,28},{28,0},{1,5},{5... | collective-permute-start | bytes 4227080 | tf_op jit(solution)/shard_map/ppermute | solution.py:17
  (103 other events, 567.5 us)
Sparse Core Ops, SparseCore 0:
  204.4 54.5 all-reduce.40
  263.1 103.2 all-reduce.36
  519.1 51.0 all-reduce.38
  574.0 125.0 all-reduce.34
